TPU v7x, 32 devices: a whole 2x2x4 slice. The times are simulated.
32 devices in a mesh: ctx: 4 (over y, x), head: 4 (over z), rep: 2 (over core).
Axes of the slice: x: 2, y: 2, z: 4, core: 2. Of those that a mesh axis runs over, the one named last changes fastest.
Arguments:
- queries: bfloat16 [512, 3072], P(('rep', 'ctx'), 'head'), parts along dimension 0, may hold values from -18 to 18
- kv_latent: bfloat16 [512, 576], P(('rep', 'ctx')), parts along dimension 0, may hold values from -140 to 140
- doc_ids: int32 [512], P(('rep', 'ctx')), parts along dimension 0, may hold values from 0 to 3, never falling along the last dimension, each value on 1 to 128 neighbouring positions
- w_kv: bfloat16 [512, 4096], P(None, 'head'), may hold values from -0.25 to 0.25
- w_out: bfloat16 [2048, 7168], P('head'), may hold values from -0.5 to 0.5
- w_enc: bfloat16 [7168, 576], P('head'), may hold values from -0.0625 to 0.0625
- residual: bfloat16 [512, 7168], P(('rep', 'ctx'), 'head'), parts along dimension 0, may hold values from -32 to 32
- norm_gain: float32 [7168], P('head'), may hold values from 0.1 to 1.9
Outputs:
- attn_out: bfloat16 [512, 7168], P(('rep', 'ctx'), 'head'), parts along dimension 0
- next_latent: bfloat16 [512, 576], P(('rep', 'ctx')), parts along dimension 0
There are 2 independent parts, one for each index of `rep`. A program takes and returns all parts, laid end to end along the dimension named above; an argument that names none is the same for every part. Nothing has to cross between parts.
Inputs may be any that keep to these rules, and one draw needn't show every extreme that they name: `doc_ids`: never falls along the window; every document number of 0 to 3 occurs, a document spans 1 to 128 tokens and one spans exactly 128.
All inputs are finite; a program needn't handle non-finite values.
Results may differ from a plain program's by a relative error of at most 0.0082.
Values may be sent and summed in bfloat16 or wider, within the bound.
A program may use at most 64 MiB of HBM per device.

v0:
```python
import functools
import math

import jax
import jax.numpy as jnp
from jax import lax
from jax.experimental import pallas as pl
from jax.experimental.pallas import tpu as pltpu
from jax.sharding import PartitionSpec as P

D = 7168
KVL = 512
ROPE = 64
NOPE = 128
VDIM = 128

LANES = 128
CHUNKS = 7
VMEM_BYTES = 60 * 1024 * 1024
MESH = pl.DeviceIdType.MESH

masked_score = -1e30
epsilon = 1e-06


def kernel(
    n_ctx, n_head, chunks,
    q_hbm, lat_hbm, doc_hbm, wkv_hbm, wout_hbm, wenc_hbm, res_hbm, gain_hbm,
    attn_ref, next_ref,
    q_v, lat_v, doc_v, wkv_v, wout_v, wenc_v, res_v, gain_v,
    lat_all, att_v, s1, r1, s2, r2, enc_s, enc_r, nl_all,
    load_sem, wout_sem, lat_send, lat_recv, s1_send, s1_recv, s2_send, s2_recv,
    enc_send, enc_recv, nl_send, nl_recv,
):
    rows = q_hbm.shape[0]
    heads = wkv_hbm.shape[1] // (NOPE + VDIM)
    width = res_hbm.shape[1]
    part = width // chunks
    piece = rows // n_head
    count = n_ctx * rows
    c = lax.axis_index("ctx")
    h = lax.axis_index("head")
    half = n_head // 2
    near = h + 1 - 2 * lax.rem(h, 2)
    far = lax.rem(h + half, n_head)
    near_far = lax.rem(near + half, n_head)
    slices = (near_far, near, far, h)

    loads = []
    for i, (src, dst) in enumerate((
        (lat_hbm, lat_v), (doc_hbm, doc_v), (q_hbm, q_v), (wkv_hbm, wkv_v),
        (res_hbm, res_v), (wenc_hbm, wenc_v), (gain_hbm, gain_v),
    )):
        loads.append(pltpu.make_async_copy(src, dst, load_sem.at[i]))
    for i in range(4):
        loads[i].start()

    barrier = pltpu.get_barrier_semaphore()
    for step in range(1, n_ctx):
        pl.semaphore_signal(barrier, inc=1, device_id={"ctx": lax.rem(c + step, n_ctx)}, device_id_type=MESH)
    for step in range(1, n_head):
        pl.semaphore_signal(barrier, inc=1, device_id={"head": lax.rem(h + step, n_head)}, device_id_type=MESH)

    wout_loads = []
    for role in range(4):
        for k in range(chunks):
            start = pl.multiple_of(slices[role] * width + k * part, LANES)
            wout_loads.append(pltpu.make_async_copy(
                wout_hbm.at[:, pl.ds(start, part)], wout_v.at[role * chunks + k], wout_sem.at[role * chunks + k]
            ))
            wout_loads[-1].start()
    for i in range(4, 7):
        loads[i].start()

    loads[0].wait()
    loads[1].wait()
    doc_row = jnp.broadcast_to(doc_v[...].astype(jnp.float32), (rows, rows))
    eye = lax.broadcasted_iota(jnp.int32, (rows, rows), 0) == lax.broadcasted_iota(jnp.int32, (rows, rows), 1)
    doc_col = jnp.sum(jnp.where(eye, doc_row, 0.0), axis=1, keepdims=True)
    lat_all[c, :, KVL:] = jnp.broadcast_to(doc_col, (rows, LANES)).astype(jnp.bfloat16)
    lat_all[c, :, : KVL + ROPE] = lat_v[...]
    for src in range(1, n_ctx):
        @pl.when(src > c)
        def _():
            lat_all[src] = jnp.zeros((rows, KVL + LANES), jnp.bfloat16)

    pl.semaphore_wait(barrier, n_ctx - 1 + n_head - 1)

    def latent_copy(step, sender):
        return pltpu.make_async_remote_copy(
            src_ref=lat_all.at[sender], dst_ref=lat_all.at[sender],
            send_sem=lat_send.at[step], recv_sem=lat_recv.at[step],
            device_id={"ctx": lax.rem(c + step, n_ctx)}, device_id_type=MESH,
        )

    for step in range(1, n_ctx):
        @pl.when(c + step < n_ctx)
        def _():
            latent_copy(step, c).start()

    loads[2].wait()
    lane = lax.broadcasted_iota(jnp.int32, (rows, LANES), 1)
    low = lane < ROPE
    q_nope, q_rope = [], []
    for head in range(heads):
        first, shift = divmod(head * (NOPE + ROPE), LANES)
        a = q_v[:, first * LANES : (first + 1) * LANES].astype(jnp.float32)
        b = q_v[:, (first + 1) * LANES : (first + 2) * LANES].astype(jnp.float32)
        if shift:
            a = pltpu.roll(a, shift, 1)
            b = pltpu.roll(b, shift, 1)
            a = jnp.where(low, a, b)
        q_nope.append(a.astype(jnp.bfloat16))
        q_rope.append(jnp.where(low, b, 0.0).astype(jnp.bfloat16))
    loads[3].wait()

    for step in range(1, n_ctx):
        @pl.when(c >= step)
        def _():
            latent_copy(step, lax.rem(c + n_ctx - step, n_ctx)).wait_recv()

    content = lat_all[:, :, :KVL].reshape(count, KVL)
    tail = lat_all[:, :, KVL:].reshape(count, LANES)
    nt = (((1,), (1,)), ((), ()))
    pick = (lax.broadcasted_iota(jnp.int32, (16, LANES), 1) == ROPE).astype(jnp.float32).astype(jnp.bfloat16)
    key_docs = lax.dot_general(pick, tail, nt, preferred_element_type=jnp.float32)[0:1]
    key_pos = lax.broadcasted_iota(jnp.int32, (rows, count), 1)
    row_pos = lax.broadcasted_iota(jnp.int32, (rows, count), 0) + c * rows
    visible = (jnp.broadcast_to(key_docs, (rows, count)) == jnp.broadcast_to(doc_col, (rows, count))) & (key_pos <= row_pos)
    score_scale = 1.0 / math.sqrt(NOPE + ROPE)
    both = NOPE + VDIM
    for head in range(heads):
        kv = jnp.dot(
            content, wkv_v[:, head * both : (head + 1) * both], preferred_element_type=jnp.float32
        ).astype(jnp.bfloat16)
        scores = lax.dot_general(q_nope[head], kv[:, :NOPE], nt, preferred_element_type=jnp.float32)
        scores = scores + lax.dot_general(q_rope[head], tail, nt, preferred_element_type=jnp.float32)
        scores = jnp.where(visible, scores * score_scale, masked_score)
        highest = jnp.max(scores, axis=1, keepdims=True)
        probs = jnp.where(visible, jnp.exp(scores - highest), 0.0)
        total = jnp.sum(probs, axis=1, keepdims=True)
        mixed = jnp.dot(probs.astype(jnp.bfloat16), kv[:, NOPE:], preferred_element_type=jnp.float32)
        att_v[:, head * VDIM : (head + 1) * VDIM] = (mixed / total).astype(jnp.bfloat16)

    att = att_v[...]

    def partial_of(role, k):
        slot = role * chunks + k
        wout_loads[slot].wait()
        return jnp.dot(att, wout_v[slot], preferred_element_type=jnp.float32)

    first = []
    for role in range(2):
        for k in range(chunks):
            slot = role * chunks + k
            s1[slot] = partial_of(role, k).astype(jnp.bfloat16)
            copy = pltpu.make_async_remote_copy(
                src_ref=s1.at[slot], dst_ref=r1.at[slot],
                send_sem=s1_send.at[slot], recv_sem=s1_recv.at[slot],
                device_id={"head": near}, device_id_type=MESH,
            )
            copy.start()
            first.append(copy)

    second = []
    for k in range(chunks):
        mine = partial_of(2, k)
        first[k].wait_recv()
        s2[k] = (mine + r1[k].astype(jnp.float32)).astype(jnp.bfloat16)
        copy = pltpu.make_async_remote_copy(
            src_ref=s2.at[k], dst_ref=r2.at[k],
            send_sem=s2_send.at[k], recv_sem=s2_recv.at[k],
            device_id={"head": far}, device_id_type=MESH,
        )
        copy.start()
        second.append(copy)

    for i in range(4, 7):
        loads[i].wait()
    encoded = jnp.zeros((rows, KVL + ROPE), jnp.float32)
    squares = jnp.zeros((rows, 1), jnp.float32)
    for k in range(chunks):
        cols = slice(k * part, (k + 1) * part)
        mine = partial_of(3, k)
        first[chunks + k].wait_recv()
        mine = mine + r1[chunks + k].astype(jnp.float32)
        second[k].wait_recv()
        out = (mine + r2[k].astype(jnp.float32)).astype(jnp.bfloat16)
        attn_ref[:, cols] = out
        hidden = res_v[:, cols].astype(jnp.float32) + out.astype(jnp.float32)
        squares = squares + jnp.sum(hidden * hidden, axis=1, keepdims=True)
        scaled = (hidden * gain_v[cols][None]).astype(jnp.bfloat16)
        encoded = encoded + lax.dot_general(
            scaled, wenc_v[:, cols], nt, preferred_element_type=jnp.float32
        )

    coarse = squares.astype(jnp.bfloat16).astype(jnp.float32)
    fine = squares - coarse
    split = ROPE + (LANES - ROPE) // 2
    sums = jnp.where(lane < split, jnp.broadcast_to(coarse, (rows, LANES)), jnp.broadcast_to(fine, (rows, LANES)))
    enc_s[:, :, KVL:] = sums.astype(jnp.bfloat16).reshape(n_head, piece, LANES)
    enc_s[:, :, : KVL + ROPE] = encoded.astype(jnp.bfloat16).reshape(n_head, piece, KVL + ROPE)
    enc_copies = []
    for step in range(1, n_head):
        peer = lax.rem(h + step, n_head)
        copy = pltpu.make_async_remote_copy(
            src_ref=enc_s.at[peer], dst_ref=enc_r.at[step - 1],
            send_sem=enc_send.at[step - 1], recv_sem=enc_recv.at[step - 1],
            device_id={"head": peer}, device_id_type=MESH,
        )
        copy.start()
        enc_copies.append(copy)
    whole = enc_s[h].astype(jnp.float32)
    for step in range(1, n_head):
        enc_copies[step - 1].wait_recv()
        whole = whole + enc_r[step - 1].astype(jnp.float32)
    square_sum = whole[:, KVL + ROPE : KVL + ROPE + 1] + whole[:, KVL + split : KVL + split + 1]
    scale = lax.rsqrt(square_sum / (width * n_head) + epsilon)
    nl_all[h] = (whole[:, : KVL + ROPE] * scale).astype(jnp.bfloat16)
    nl_copies = []
    for step in range(1, n_head):
        copy = pltpu.make_async_remote_copy(
            src_ref=nl_all.at[h], dst_ref=nl_all.at[h],
            send_sem=nl_send.at[step - 1], recv_sem=nl_recv.at[step - 1],
            device_id={"head": lax.rem(h + step, n_head)}, device_id_type=MESH,
        )
        copy.start()
        nl_copies.append(copy)
    for copy in nl_copies:
        copy.wait_recv()
    next_ref[...] = nl_all[...].reshape(rows, KVL + ROPE)

    for step in range(1, n_ctx):
        @pl.when(c + step < n_ctx)
        def _():
            latent_copy(step, c).wait_send()
    for copy in first + second + enc_copies + nl_copies:
        copy.wait_send()


def fused(n_ctx, n_head, queries, kv_latent, doc_ids, w_kv, w_out, w_enc, residual, norm_gain):
    rows = queries.shape[0]
    heads = w_kv.shape[1] // (NOPE + VDIM)
    width = residual.shape[1]
    part = width // CHUNKS
    piece = rows // n_head
    bf16, f32 = jnp.bfloat16, jnp.float32
    hbm = pl.BlockSpec(memory_space=pltpu.HBM)
    vmem = pl.BlockSpec(memory_space=pltpu.VMEM)
    dma = pltpu.SemaphoreType.DMA
    return pl.pallas_call(
        functools.partial(kernel, n_ctx, n_head, CHUNKS),
        out_shape=(pltpu.VMEM((rows, width), bf16), pltpu.VMEM((rows, KVL + ROPE), bf16)),
        in_specs=[hbm] * 8,
        out_specs=(vmem, vmem),
        scratch_shapes=[
            pltpu.VMEM(queries.shape, bf16),
            pltpu.VMEM(kv_latent.shape, bf16),
            pltpu.VMEM((1, rows), jnp.int32),
            pltpu.VMEM(w_kv.shape, bf16),
            pltpu.VMEM((4 * CHUNKS, w_out.shape[0], part), bf16),
            pltpu.VMEM(w_enc.shape[::-1], bf16),
            pltpu.VMEM(residual.shape, bf16),
            pltpu.VMEM((width,), f32),
            pltpu.VMEM((n_ctx, rows, KVL + LANES), bf16),
            pltpu.VMEM((rows, heads * VDIM), bf16),
            pltpu.VMEM((2 * CHUNKS, rows, part), bf16),
            pltpu.VMEM((2 * CHUNKS, rows, part), bf16),
            pltpu.VMEM((CHUNKS, rows, part), bf16),
            pltpu.VMEM((CHUNKS, rows, part), bf16),
            pltpu.VMEM((n_head, piece, KVL + LANES), bf16),
            pltpu.VMEM((n_head - 1, piece, KVL + LANES), bf16),
            pltpu.VMEM((n_head, piece, KVL + ROPE), bf16),
            dma((7,)),
            dma((4 * CHUNKS,)),
            dma((n_ctx,)),
            dma((n_ctx,)),
            dma((2 * CHUNKS,)),
            dma((2 * CHUNKS,)),
            dma((CHUNKS,)),
            dma((CHUNKS,)),
            dma((n_head - 1,)),
            dma((n_head - 1,)),
            dma((n_head - 1,)),
            dma((n_head - 1,)),
        ],
        compiler_params=pltpu.CompilerParams(
            collective_id=0, has_side_effects=True, vmem_limit_bytes=VMEM_BYTES
        ),
        name="latent_layer",
    )(
        queries, kv_latent, doc_ids[None], w_kv, w_out, w_enc.T, residual, norm_gain,
    )


def general(n_ctx, n_head, queries, kv_latent, doc_ids, w_kv, w_out, w_enc, residual, norm_gain):
    rows_here = queries.shape[0]
    heads_here = w_kv.shape[1] // (NOPE + VDIM)
    query_heads = queries.reshape(rows_here, heads_here, NOPE + ROPE)
    q_nope = query_heads[:, :, :NOPE]
    q_rope = query_heads[:, :, NOPE:]
    positions = lax.axis_index("ctx") * rows_here + lax.iota(jnp.int32, rows_here)
    weights = w_kv.reshape(KVL, heads_here, NOPE + VDIM)
    f32 = jnp.float32
    latents = lax.all_gather(kv_latent, "ctx", axis=0, tiled=True)
    key_docs = lax.all_gather(doc_ids, "ctx", axis=0, tiled=True)
    key_pos = lax.iota(jnp.int32, latents.shape[0])
    content = latents[:, :KVL]
    rotary = latents[:, KVL:]
    both = jnp.einsum("nc,chd->nhd", content, weights, preferred_element_type=f32).astype(jnp.bfloat16)
    keys = both[:, :, :NOPE]
    values = both[:, :, NOPE:]
    scores = jnp.einsum("qhd,nhd->hqn", q_nope, keys, preferred_element_type=f32)
    scores = scores + jnp.einsum("qhd,nd->hqn", q_rope, rotary, preferred_element_type=f32)
    visible = (key_docs[None, :] == doc_ids[:, None]) & (key_pos[None, :] <= positions[:, None])
    scores = jnp.where(visible[None], scores * (1.0 / math.sqrt(NOPE + ROPE)), masked_score)
    highest = jnp.max(scores, axis=2)
    probs = jnp.where(visible[None], jnp.exp(scores - highest[:, :, None]), 0.0)
    total = jnp.sum(probs, axis=2)
    mixed = jnp.einsum("hqn,nhd->hqd", probs.astype(jnp.bfloat16), values, preferred_element_type=f32)
    attended = (mixed / total[:, :, None]).astype(jnp.bfloat16)
    side_by_side = attended.transpose(1, 0, 2).reshape(rows_here, heads_here * VDIM)
    summed = lax.psum_scatter(
        lax.dot_general(w_out, side_by_side, (((0,), (1,)), ((), ())), preferred_element_type=f32),
        "head", scatter_dimension=0, tiled=True,
    )
    attn_out = summed.T.astype(jnp.bfloat16)
    hidden = residual.astype(f32) + attn_out.astype(f32)
    squares = jnp.sum(hidden * hidden, axis=1)
    scaled = (hidden * norm_gain[None, :]).astype(jnp.bfloat16)
    encoded = jnp.dot(scaled, w_enc, preferred_element_type=f32)
    enc_sum, sq_sum = lax.psum((encoded, squares), "head")
    next_latent = (enc_sum * lax.rsqrt(sq_sum / D + epsilon)[:, None]).astype(jnp.bfloat16)
    return (attn_out, next_latent)


def per_device(n_ctx, n_head, *args):
    rows, width = args[6].shape
    whole_tiles = width % (CHUNKS * LANES) == 0 and rows % (16 * n_head) == 0
    body = fused if n_head == 4 and whole_tiles else general
    return body(n_ctx, n_head, *args)


def solution(mesh):
    return jax.shard_map(
        functools.partial(per_device, mesh.shape["ctx"], mesh.shape["head"]),
        mesh=mesh,
        in_specs=(
            P(("rep", "ctx"), "head"),
            P(("rep", "ctx"), None),
            P(("rep", "ctx")),
            P(None, "head"),
            P("head", None),
            P("head", None),
            P(("rep", "ctx"), "head"),
            P("head"),
        ),
        out_specs=(P(("rep", "ctx"), "head"), P(("rep", "ctx"), None)),
        check_vma=False,
    )
```

profile of v0, /device:TPU:4, one launch (start us, length us, event | category | flops | bytes accessed | tf_op | source)
XLA Modules:
  0.0 38.5 jit_solution(9012582616130123079)
XLA Ops:
  0.6 36.5 %latent_layer.1 = (bf16[64,1792]{1,0:T(8,128)(2,1)S(1)}, bf16[64,576]{1,0:T(8,128)(2,1)S(1)}) custom-call(bf16[64,768]{1,0:T(8,128)(2,1)} %q_hbm.1, bf16[64,576]{1,0:T(8,128)(2,1)} %lat_hbm.1, s32[1,64]{1,0:T(1,128)} %bitcast.3, bf16[512,1024]{1,0:T(8,128)(2,1)} %wkv_hbm.1, bf16[512,7168]{1,0:T(8,128)(2,1)} %wout_hbm.1, bf16[576,1792]{1,0:T(8,128)(2,1)} %bitcast.2, ...), custom_call_target="tpu_custom_call" | custom-call | tf_op jit(solution)/shard_map/latent_layer/pallas_call | solution.py:251
  37.1 0.7 %copy.12 = bf16[64,1792]{1,0:T(8,128)(2,1)} copy(bf16[64,1792]{1,0:T(8,128)(2,1)S(1)} %get-tuple-element.2) | data formatting | bytes 458752
  37.8 0.6 %copy.13 = bf16[64,576]{1,0:T(8,128)(2,1)} copy(bf16[64,576]{1,0:T(8,128)(2,1)S(1)} %get-tuple-element.3) | data formatting | bytes 147456
where the time goes:
time: 38.6 us; the launch traced here: 38.5 us
  Pallas kernels  36.5 us (95%)
  local copies, waits for them, and re-layouts  1.33 us (3%)
  between operations  0.64 us (2%)
    pallas_call x1, Pallas kernels, fused(): pl.pallas_call(functools.partial(kernel, n_ctx, n_head, CHUNKS), out_shap...  36.5 us
    unnamed x2, local copies, waits for them, and re-layouts  1.33 us

commit v1 on v0

v1 whole, which is shorter than its diff:
```python
import functools
import math

import jax
import jax.numpy as jnp
from jax import lax
from jax.experimental import pallas as pl
from jax.experimental.pallas import tpu as pltpu
from jax.sharding import PartitionSpec as P

D = 7168
KVL = 512
ROPE = 64
NOPE = 128
VDIM = 128

LANES = 128
CHUNKS = 7
PIECE = 16
VMEM_BYTES = 60 * 1024 * 1024
MESH = pl.DeviceIdType.MESH

masked_score = -1e30
epsilon = 1e-06


def kernel(
    n_ctx, n_head, back, chunks,
    q_hbm, lat_hbm, doc_hbm, wkv_hbm, wout_hbm, wenc_hbm, res_hbm, gain_hbm,
    attn_ref, next_ref,
    q_v, lat_v, doc_v, wkv_v, wout_v, wenc_v, res_v, gain_v,
    lat_all, att_v, sums_s, sums_r, enc_s, enc_r,
    load_sem, wout_sem, lat_send, lat_recv, sums_send, sums_recv,
    enc_send, enc_recv,
):
    rows = q_hbm.shape[0]
    heads = wkv_hbm.shape[1] // (NOPE + VDIM)
    width = res_hbm.shape[1]
    part = width // chunks
    pieces = rows // PIECE
    c = lax.axis_index("ctx")
    h = lax.axis_index("head")
    side = h // 2
    end, mate = 3 * side, 1 + side
    partner = h + 1 - 2 * lax.rem(h, 2)
    other = 3 - mate
    at_end = h == end
    at_mate = h == mate
    far_end = 3 - end
    slices = (far_end, other, partner, h)

    loads = []
    for i, (src, dst) in enumerate((
        (lat_hbm, lat_v), (doc_hbm, doc_v), (q_hbm, q_v), (wkv_hbm, wkv_v),
        (res_hbm, res_v), (wenc_hbm, wenc_v), (gain_hbm, gain_v),
    )):
        loads.append(pltpu.make_async_copy(src, dst, load_sem.at[i]))
    for i in range(4):
        loads[i].start()

    barrier = pltpu.get_barrier_semaphore()
    near = [("ctx", c, step, n_ctx) for step in range(1, back + 1)] + [("head", h, 1, n_head)]
    for axis, here, step, count in near:
        @pl.when(here + step < count)
        def _():
            pl.semaphore_signal(barrier, inc=1, device_id={axis: here + step}, device_id_type=MESH)

        @pl.when(here >= step)
        def _():
            pl.semaphore_signal(barrier, inc=1, device_id={axis: here - step}, device_id_type=MESH)

    for role in range(4):
        for k in range(chunks):
            start = pl.multiple_of(slices[role] * width + k * part, LANES)
            pltpu.make_async_copy(
                wout_hbm.at[:, pl.ds(start, part)], wout_v.at[role, k], wout_sem.at[role]
            ).start()
    for i in range(4, 7):
        loads[i].start()

    loads[0].wait()
    loads[1].wait()
    docs_here = doc_v[...].astype(jnp.float32)
    row_of = lax.broadcasted_iota(jnp.int32, (rows, rows), 0)
    col_of = lax.broadcasted_iota(jnp.int32, (rows, rows), 1)
    doc_col = jnp.sum(
        jnp.where(row_of == col_of, jnp.broadcast_to(docs_here, (rows, rows)), 0.0), axis=1, keepdims=True
    )
    lat_all[back, :, KVL:] = jnp.broadcast_to(doc_col, (rows, LANES)).astype(jnp.bfloat16)
    lat_all[back, :, : KVL + ROPE] = lat_v[...]
    for step in range(1, back + 1):
        @pl.when(c < step)
        def _():
            lat_all[back - step] = jnp.zeros((rows, KVL + LANES), jnp.bfloat16)

    peers = 0
    for axis, here, step, count in near:
        peers = peers + (here + step < count).astype(jnp.int32) + (here >= step).astype(jnp.int32)
    pl.semaphore_wait(barrier, peers)

    def latent_copy(step):
        return pltpu.make_async_remote_copy(
            src_ref=lat_all.at[back], dst_ref=lat_all.at[back - step],
            send_sem=lat_send.at[step - 1], recv_sem=lat_recv.at[step - 1],
            device_id={"ctx": lax.rem(c + step, n_ctx)}, device_id_type=MESH,
        )

    for step in range(1, back + 1):
        @pl.when(c + step < n_ctx)
        def _():
            latent_copy(step).start()

    loads[2].wait()
    low = lax.broadcasted_iota(jnp.int32, (rows, LANES), 1) < ROPE
    query = []
    for head in range(heads):
        first, shift = divmod(head * (NOPE + ROPE), LANES)
        a = q_v[:, first * LANES : (first + 1) * LANES].astype(jnp.float32)
        b = q_v[:, (first + 1) * LANES : (first + 2) * LANES].astype(jnp.float32)
        if shift:
            a = pltpu.roll(a, shift, 1)
            b = pltpu.roll(b, shift, 1)
            a = jnp.where(low, a, b)
        query.append(jnp.concatenate([a, jnp.where(low, b, 0.0)], axis=1).astype(jnp.bfloat16))
    loads[3].wait()

    nt = (((1,), (1,)), ((), ()))
    score_scale = 1.0 / math.sqrt(NOPE + ROPE)
    both = NOPE + VDIM

    def expand(latent):
        return jnp.dot(latent, wkv_v[...], preferred_element_type=jnp.float32).astype(jnp.bfloat16)

    def score(expanded, tail, visible):
        found = []
        for head in range(heads):
            keys = jnp.concatenate([expanded[:, head * both : head * both + NOPE], tail], axis=1)
            one = lax.dot_general(query[head], keys, nt, preferred_element_type=jnp.float32)
            found.append(jnp.where(visible, one * score_scale, masked_score))
        return found

    seen_own = (jnp.broadcast_to(docs_here, (rows, rows)) == jnp.broadcast_to(doc_col, (rows, rows))) & (col_of <= row_of)
    kv_own = expand(lat_v[:, :KVL])
    own = score(kv_own, lat_all[back, :, KVL:], seen_own)

    for step in range(1, back + 1):
        @pl.when(c >= step)
        def _():
            latent_copy(step).wait_recv()

    count = back * rows
    tail_prev = lat_all[:back, :, KVL:].reshape(count, LANES)
    pick = (lax.broadcasted_iota(jnp.int32, (16, LANES), 1) == ROPE).astype(jnp.float32).astype(jnp.bfloat16)
    key_docs = lax.dot_general(pick, tail_prev, nt, preferred_element_type=jnp.float32)[0:1]
    exists = lax.broadcasted_iota(jnp.int32, (rows, count), 1) + (c - back) * rows >= 0
    seen_prev = (jnp.broadcast_to(key_docs, (rows, count)) == jnp.broadcast_to(doc_col, (rows, count))) & exists
    kv_prev = expand(lat_all[:back, :, :KVL].reshape(count, KVL))
    prev = score(kv_prev, tail_prev, seen_prev)
    for head in range(heads):
        highest = jnp.maximum(
            jnp.max(own[head], axis=1, keepdims=True), jnp.max(prev[head], axis=1, keepdims=True)
        )
        p_own = jnp.where(seen_own, jnp.exp(own[head] - highest), 0.0)
        p_prev = jnp.where(seen_prev, jnp.exp(prev[head] - highest), 0.0)
        total = jnp.sum(p_own, axis=1, keepdims=True) + jnp.sum(p_prev, axis=1, keepdims=True)
        columns = slice(head * both + NOPE, (head + 1) * both)
        mixed = jnp.dot(p_own.astype(jnp.bfloat16), kv_own[:, columns], preferred_element_type=jnp.float32)
        mixed = mixed + jnp.dot(p_prev.astype(jnp.bfloat16), kv_prev[:, columns], preferred_element_type=jnp.float32)
        att_v[:, head * VDIM : (head + 1) * VDIM] = (mixed / total).astype(jnp.bfloat16)

    def partial_of(role, k):
        if k == 0:
            pltpu.make_async_copy(wout_v.at[role], wout_v.at[role], wout_sem.at[role]).wait()
        return jnp.dot(att_v[...], wout_v[role, k], preferred_element_type=jnp.float32)

    def sums_copy(slot, landing, device):
        return pltpu.make_async_remote_copy(
            src_ref=sums_s.at[slot], dst_ref=sums_r.at[landing],
            send_sem=sums_send, recv_sem=sums_recv.at[landing],
            device_id={"head": device}, device_id_type=MESH,
        )

    def piece_copy(piece, landing, device):
        return pltpu.make_async_remote_copy(
            src_ref=enc_s.at[piece], dst_ref=enc_r.at[landing],
            send_sem=enc_send, recv_sem=enc_recv.at[landing],
            device_id={"head": device}, device_id_type=MESH,
        )

    def finish(k, out, encoded, squares):
        cols = slice(k * part, (k + 1) * part)
        attn_ref[:, cols] = out
        hidden = res_v[:, cols].astype(jnp.float32) + out.astype(jnp.float32)
        squares = squares + jnp.sum(hidden * hidden, axis=1, keepdims=True)
        scaled = (hidden * gain_v[cols][None]).astype(jnp.bfloat16)
        encoded = encoded + lax.dot_general(scaled, wenc_v[:, cols], nt, preferred_element_type=jnp.float32)
        return encoded, squares

    split = ROPE + (LANES - ROPE) // 2
    coarse_lanes = lax.broadcasted_iota(jnp.int32, (PIECE, LANES), 1) < split

    def pack(piece, encoded, squares):
        coarse = squares.astype(jnp.bfloat16).astype(jnp.float32)
        sums = jnp.where(
            coarse_lanes,
            jnp.broadcast_to(coarse, (PIECE, LANES)), jnp.broadcast_to(squares - coarse, (PIECE, LANES)),
        )
        enc_s[piece, :, KVL:] = sums.astype(jnp.bfloat16)
        enc_s[piece, :, : KVL + ROPE] = encoded.astype(jnp.bfloat16)

    def unpack(packed):
        squares = packed[:, KVL + ROPE : KVL + ROPE + 1] + packed[:, KVL + split : KVL + split + 1]
        return packed[:, : KVL + ROPE], squares

    def conclude(near_half):
        for piece in range(pieces):
            if near_half is None:
                piece_copy(piece, piece, partner).wait_recv()
            piece_copy(piece, pieces + piece, other).wait_recv()
            near = (enc_r[piece] if near_half is None else near_half[piece]).astype(jnp.float32)
            whole, square_sum = unpack(near + enc_r[pieces + piece].astype(jnp.float32))
            scale = lax.rsqrt(square_sum / (width * n_head) + epsilon)
            next_ref[piece * PIECE : (piece + 1) * PIECE, :] = (whole * scale).astype(jnp.bfloat16)

    for i in range(4, 7):
        loads[i].wait()
    nothing = jnp.zeros((rows, KVL + ROPE), jnp.float32), jnp.zeros((rows, 1), jnp.float32)

    @pl.when(at_end)
    def _():
        for slot in range(3 * chunks):
            role, k = divmod(slot, chunks)
            sums_s[slot] = partial_of(role, k).astype(jnp.bfloat16)
            sums_copy(slot, slot, partner).start()
        encoded, squares = nothing
        for k in range(chunks):
            mine = partial_of(3, k)
            sums_copy(k, k, partner).wait_recv()
            out = (mine + sums_r[k].astype(jnp.float32)).astype(jnp.bfloat16)
            encoded, squares = finish(k, out, encoded, squares)
        for piece in range(pieces):
            own_rows = slice(piece * PIECE, (piece + 1) * PIECE)
            pack(piece, encoded[own_rows], squares[own_rows])
            piece_copy(piece, piece, partner).start()
        conclude(None)

    @pl.when(at_mate)
    def _():
        lag = 3
        for slot in range(2 * chunks):
            role, k = divmod(slot, chunks)
            mine = partial_of(role, k)
            sums_copy(slot, slot, partner).wait_recv()
            sums_s[slot] = (mine + sums_r[slot].astype(jnp.float32)).astype(jnp.bfloat16)
            sums_copy(slot, 3 * chunks + slot, other).start()
            k = slot - lag
            if 0 <= k < chunks:
                mine = partial_of(2, k)
                landed = 3 * chunks + k
                sums_copy(k, landed, other).wait_recv()
                sums_s[2 * chunks + k] = (mine + sums_r[landed].astype(jnp.float32)).astype(jnp.bfloat16)
                sums_copy(2 * chunks + k, k, partner).start()
        encoded, squares = nothing
        for k in range(chunks):
            mine = partial_of(3, k)
            landed = 4 * chunks + k
            sums_copy(k, landed, other).wait_recv()
            mine = mine + sums_r[landed].astype(jnp.float32)
            sums_copy(k, 2 * chunks + k, partner).wait_recv()
            out = (mine + sums_r[2 * chunks + k].astype(jnp.float32)).astype(jnp.bfloat16)
            encoded, squares = finish(k, out, encoded, squares)
        for piece in range(pieces):
            own_rows = slice(piece * PIECE, (piece + 1) * PIECE)
            piece_copy(piece, piece, partner).wait_recv()
            theirs, their_squares = unpack(enc_r[piece].astype(jnp.float32))
            pack(piece, encoded[own_rows] + theirs, squares[own_rows] + their_squares)
            piece_copy(piece, pieces + piece, far_end).start()
            piece_copy(piece, piece, partner).start()
        for piece in range(pieces):
            piece_copy(piece, pieces + piece, other).start()
        conclude(enc_s)

    for step in range(1, back + 1):
        @pl.when(c + step < n_ctx)
        def _():
            latent_copy(step).wait_send()
    all_sums = pltpu.make_async_copy(sums_s, sums_s, sums_send)
    all_sums.wait()
    all_pieces = pltpu.make_async_copy(enc_s, enc_s, enc_send)

    @pl.when(at_end)
    def _():
        all_pieces.wait()

    @pl.when(at_mate)
    def _():
        for _ in range(3):
            all_pieces.wait()


def fused(n_ctx, n_head, queries, kv_latent, doc_ids, w_kv, w_out, w_enc, residual, norm_gain):
    rows = queries.shape[0]
    heads = w_kv.shape[1] // (NOPE + VDIM)
    width = residual.shape[1]
    part = width // CHUNKS
    pieces = rows // PIECE
    back = min(n_ctx - 1, -(-(n_ctx * rows // 2 - 1) // rows))
    bf16, f32 = jnp.bfloat16, jnp.float32
    hbm = pl.BlockSpec(memory_space=pltpu.HBM)
    vmem = pl.BlockSpec(memory_space=pltpu.VMEM)
    dma = pltpu.SemaphoreType.DMA
    return pl.pallas_call(
        functools.partial(kernel, n_ctx, n_head, back, CHUNKS),
        out_shape=(pltpu.VMEM((rows, width), bf16), pltpu.VMEM((rows, KVL + ROPE), bf16)),
        in_specs=[hbm] * 8,
        out_specs=(vmem, vmem),
        scratch_shapes=[
            pltpu.VMEM(queries.shape, bf16),
            pltpu.VMEM(kv_latent.shape, bf16),
            pltpu.VMEM((1, rows), jnp.int32),
            pltpu.VMEM(w_kv.shape, bf16),
            pltpu.VMEM((4, CHUNKS, w_out.shape[0], part), bf16),
            pltpu.VMEM(w_enc.shape[::-1], bf16),
            pltpu.VMEM(residual.shape, bf16),
            pltpu.VMEM((width,), f32),
            pltpu.VMEM((back + 1, rows, KVL + LANES), bf16),
            pltpu.VMEM((rows, heads * VDIM), bf16),
            pltpu.VMEM((3 * CHUNKS, rows, part), bf16),
            pltpu.VMEM((5 * CHUNKS, rows, part), bf16),
            pltpu.VMEM((pieces, PIECE, KVL + LANES), bf16),
            pltpu.VMEM((2 * pieces, PIECE, KVL + LANES), bf16),
            dma((7,)),
            dma((4,)),
            dma((back,)),
            dma((back,)),
            dma,
            dma((5 * CHUNKS,)),
            dma,
            dma((2 * pieces,)),
        ],
        compiler_params=pltpu.CompilerParams(
            collective_id=0, has_side_effects=True, vmem_limit_bytes=VMEM_BYTES
        ),
        name="latent_layer",
    )(
        queries, kv_latent, doc_ids[None], w_kv, w_out, w_enc.T, residual, norm_gain,
    )


def general(n_ctx, n_head, queries, kv_latent, doc_ids, w_kv, w_out, w_enc, residual, norm_gain):
    rows_here = queries.shape[0]
    heads_here = w_kv.shape[1] // (NOPE + VDIM)
    query_heads = queries.reshape(rows_here, heads_here, NOPE + ROPE)
    q_nope = query_heads[:, :, :NOPE]
    q_rope = query_heads[:, :, NOPE:]
    positions = lax.axis_index("ctx") * rows_here + lax.iota(jnp.int32, rows_here)
    weights = w_kv.reshape(KVL, heads_here, NOPE + VDIM)
    f32 = jnp.float32
    latents = lax.all_gather(kv_latent, "ctx", axis=0, tiled=True)
    key_docs = lax.all_gather(doc_ids, "ctx", axis=0, tiled=True)
    key_pos = lax.iota(jnp.int32, latents.shape[0])
    content = latents[:, :KVL]
    rotary = latents[:, KVL:]
    both = jnp.einsum("nc,chd->nhd", content, weights, preferred_element_type=f32).astype(jnp.bfloat16)
    keys = both[:, :, :NOPE]
    values = both[:, :, NOPE:]
    scores = jnp.einsum("qhd,nhd->hqn", q_nope, keys, preferred_element_type=f32)
    scores = scores + jnp.einsum("qhd,nd->hqn", q_rope, rotary, preferred_element_type=f32)
    visible = (key_docs[None, :] == doc_ids[:, None]) & (key_pos[None, :] <= positions[:, None])
    scores = jnp.where(visible[None], scores * (1.0 / math.sqrt(NOPE + ROPE)), masked_score)
    highest = jnp.max(scores, axis=2)
    probs = jnp.where(visible[None], jnp.exp(scores - highest[:, :, None]), 0.0)
    total = jnp.sum(probs, axis=2)
    mixed = jnp.einsum("hqn,nhd->hqd", probs.astype(jnp.bfloat16), values, preferred_element_type=f32)
    attended = (mixed / total[:, :, None]).astype(jnp.bfloat16)
    side_by_side = attended.transpose(1, 0, 2).reshape(rows_here, heads_here * VDIM)
    summed = lax.psum_scatter(
        lax.dot_general(w_out, side_by_side, (((0,), (1,)), ((), ())), preferred_element_type=f32),
        "head", scatter_dimension=0, tiled=True,
    )
    attn_out = summed.T.astype(jnp.bfloat16)
    hidden = residual.astype(f32) + attn_out.astype(f32)
    squares = jnp.sum(hidden * hidden, axis=1)
    scaled = (hidden * norm_gain[None, :]).astype(jnp.bfloat16)
    encoded = jnp.dot(scaled, w_enc, preferred_element_type=f32)
    enc_sum, sq_sum = lax.psum((encoded, squares), "head")
    next_latent = (enc_sum * lax.rsqrt(sq_sum / D + epsilon)[:, None]).astype(jnp.bfloat16)
    return (attn_out, next_latent)


def per_device(n_ctx, n_head, *args):
    rows, width = args[6].shape
    whole_tiles = width % (CHUNKS * LANES) == 0 and rows % PIECE == 0 and rows <= LANES
    body = fused if n_head == 4 and whole_tiles else general
    return body(n_ctx, n_head, *args)


def solution(mesh):
    return jax.shard_map(
        functools.partial(per_device, mesh.shape["ctx"], mesh.shape["head"]),
        mesh=mesh,
        in_specs=(
            P(("rep", "ctx"), "head"),
            P(("rep", "ctx"), None),
            P(("rep", "ctx")),
            P(None, "head"),
            P("head", None),
            P("head", None),
            P(("rep", "ctx"), "head"),
            P("head"),
        ),
        out_specs=(P(("rep", "ctx"), "head"), P(("rep", "ctx"), None)),
        check_vma=False,
    )
```

time: 38.6 us -> 33 us (0.85)
  Pallas kernels: 36.5 us -> 30.9 us
    pallas_call x1, Pallas kernels: 36.5 us -> 30.9 us  [fused(): pl.pallas_call(functools.partial(kernel, n_ctx, n_head, back, CHUNKS), ou...]
where the time goes in v1:
time: 33 us; the launch traced here: 32.9 us
  Pallas kernels  30.9 us (94%)
  local copies, waits for them, and re-layouts  1.33 us (4%)
  between operations  0.64 us (2%)
    pallas_call x1, Pallas kernels, fused(): pl.pallas_call(functools.partial(kernel, n_ctx, n_head, back, CHUNKS), ou...  30.9 us
    unnamed x2, local copies, waits for them, and re-layouts  1.33 us

profile of v1, /device:TPU:4, one launch (start us, length us, event | category | flops | bytes accessed | tf_op | source)
XLA Modules:
  0.0 32.9 jit_solution(194071457081810925)
XLA Ops:
  0.6 30.9 %latent_layer.1 = (bf16[64,1792]{1,0:T(8,128)(2,1)S(1)}, bf16[64,576]{1,0:T(8,128)(2,1)S(1)}) custom-call(bf16[64,768]{1,0:T(8,128)(2,1)} %q_hbm.1, bf16[64,576]{1,0:T(8,128)(2,1)} %lat_hbm.1, s32[1,64]{1,0:T(1,128)} %bitcast.3, bf16[512,1024]{1,0:T(8,128)(2,1)} %wkv_hbm.1, bf16[512,7168]{1,0:T(8,128)(2,1)} %wout_hbm.1, bf16[576,1792]{1,0:T(8,128)(2,1)} %bitcast.2, ...), custom_call_target="tpu_custom_call" | custom-call | tf_op jit(solution)/shard_map/latent_layer/pallas_call | solution.py:312
  31.5 0.7 %copy.12 = bf16[64,1792]{1,0:T(8,128)(2,1)} copy(bf16[64,1792]{1,0:T(8,128)(2,1)S(1)} %get-tuple-element.2) | data formatting | bytes 458752
  32.2 0.6 %copy.13 = bf16[64,576]{1,0:T(8,128)(2,1)} copy(bf16[64,576]{1,0:T(8,128)(2,1)S(1)} %get-tuple-element.3) | data formatting | bytes 147456

commit v2 on v1

--- a/solution.py
+++ b/solution.py
@@ -31,7 +31,7 @@
     q_v, lat_v, doc_v, wkv_v, wout_v, wenc_v, res_v, gain_v,
     lat_all, att_v, sums_s, sums_r, enc_s, enc_r,
     load_sem, wout_sem, lat_send, lat_recv, sums_send, sums_recv,
-    enc_send, enc_recv,
+    enc_send, enc_recv, far_in,
 ):
     rows = q_hbm.shape[0]
     heads = wkv_hbm.shape[1] // (NOPE + VDIM)
@@ -97,6 +97,11 @@
     for axis, here, step, count in near:
         peers = peers + (here + step < count).astype(jnp.int32) + (here >= step).astype(jnp.int32)
     pl.semaphore_wait(barrier, peers)
+
+    @pl.when(at_mate)
+    def _():
+        pl.semaphore_signal(far_in, inc=1, device_id={"head": other}, device_id_type=MESH)
+
 
     def latent_copy(step):
         return pltpu.make_async_remote_copy(
@@ -236,7 +241,9 @@
         for k in range(chunks):
             mine = partial_of(3, k)
             sums_copy(k, k, partner).wait_recv()
-            out = (mine + sums_r[k].astype(jnp.float32)).astype(jnp.bfloat16)
+            mine = mine + sums_r[k].astype(jnp.float32)
+            sums_copy(k, chunks + k, partner).wait_recv()
+            out = (mine + sums_r[chunks + k].astype(jnp.float32)).astype(jnp.bfloat16)
             encoded, squares = finish(k, out, encoded, squares)
         for piece in range(pieces):
             own_rows = slice(piece * PIECE, (piece + 1) * PIECE)
@@ -246,26 +253,24 @@
 
     @pl.when(at_mate)
     def _():
-        lag = 3
+        for k in range(chunks):
+            sums_s[2 * chunks + k] = partial_of(2, k).astype(jnp.bfloat16)
+            sums_copy(2 * chunks + k, k, partner).start()
+        pl.semaphore_wait(far_in, 1)
         for slot in range(2 * chunks):
             role, k = divmod(slot, chunks)
             mine = partial_of(role, k)
             sums_copy(slot, slot, partner).wait_recv()
             sums_s[slot] = (mine + sums_r[slot].astype(jnp.float32)).astype(jnp.bfloat16)
-            sums_copy(slot, 3 * chunks + slot, other).start()
-            k = slot - lag
-            if 0 <= k < chunks:
-                mine = partial_of(2, k)
-                landed = 3 * chunks + k
-                sums_copy(k, landed, other).wait_recv()
-                sums_s[2 * chunks + k] = (mine + sums_r[landed].astype(jnp.float32)).astype(jnp.bfloat16)
-                sums_copy(2 * chunks + k, k, partner).start()
+            if role == 0:
+                sums_copy(slot, chunks + k, far_end).start()
+            else:
+                sums_copy(slot, 3 * chunks + k, other).start()
         encoded, squares = nothing
         for k in range(chunks):
             mine = partial_of(3, k)
-            landed = 4 * chunks + k
-            sums_copy(k, landed, other).wait_recv()
-            mine = mine + sums_r[landed].astype(jnp.float32)
+            sums_copy(k, 3 * chunks + k, other).wait_recv()
+            mine = mine + sums_r[3 * chunks + k].astype(jnp.float32)
             sums_copy(k, 2 * chunks + k, partner).wait_recv()
             out = (mine + sums_r[2 * chunks + k].astype(jnp.float32)).astype(jnp.bfloat16)
             encoded, squares = finish(k, out, encoded, squares)
@@ -298,6 +303,17 @@
             all_pieces.wait()
 
 
+def write_out(attn_v, next_v, attn_hbm, next_hbm, sem):
+    copies = [
+        pltpu.make_async_copy(attn_v, attn_hbm, sem.at[0]),
+        pltpu.make_async_copy(next_v, next_hbm, sem.at[1]),
+    ]
+    for copy in copies:
+        copy.start()
+    for copy in copies:
+        copy.wait()
+
+
 def fused(n_ctx, n_head, queries, kv_latent, doc_ids, w_kv, w_out, w_enc, residual, norm_gain):
     rows = queries.shape[0]
     heads = w_kv.shape[1] // (NOPE + VDIM)
@@ -309,7 +325,7 @@
     hbm = pl.BlockSpec(memory_space=pltpu.HBM)
     vmem = pl.BlockSpec(memory_space=pltpu.VMEM)
     dma = pltpu.SemaphoreType.DMA
-    return pl.pallas_call(
+    done = pl.pallas_call(
         functools.partial(kernel, n_ctx, n_head, back, CHUNKS),
         out_shape=(pltpu.VMEM((rows, width), bf16), pltpu.VMEM((rows, KVL + ROPE), bf16)),
         in_specs=[hbm] * 8,
@@ -326,7 +342,7 @@
             pltpu.VMEM((back + 1, rows, KVL + LANES), bf16),
             pltpu.VMEM((rows, heads * VDIM), bf16),
             pltpu.VMEM((3 * CHUNKS, rows, part), bf16),
-            pltpu.VMEM((5 * CHUNKS, rows, part), bf16),
+            pltpu.VMEM((4 * CHUNKS, rows, part), bf16),
             pltpu.VMEM((pieces, PIECE, KVL + LANES), bf16),
             pltpu.VMEM((2 * pieces, PIECE, KVL + LANES), bf16),
             dma((7,)),
@@ -334,9 +350,10 @@
             dma((back,)),
             dma((back,)),
             dma,
-            dma((5 * CHUNKS,)),
+            dma((4 * CHUNKS,)),
             dma,
             dma((2 * pieces,)),
+            pltpu.SemaphoreType.REGULAR,
         ],
         compiler_params=pltpu.CompilerParams(
             collective_id=0, has_side_effects=True, vmem_limit_bytes=VMEM_BYTES
@@ -345,6 +362,14 @@
     )(
         queries, kv_latent, doc_ids[None], w_kv, w_out, w_enc.T, residual, norm_gain,
     )
+    return pl.pallas_call(
+        write_out,
+        out_shape=tuple(pltpu.HBM(one.shape, one.dtype) for one in done),
+        in_specs=[vmem] * 2,
+        out_specs=(hbm, hbm),
+        scratch_shapes=[dma((2,))],
+        name="write_out",
+    )(*[pltpu.with_memory_space_constraint(one, pltpu.VMEM) for one in done])
 
 
 def general(n_ctx, n_head, queries, kv_latent, doc_ids, w_kv, w_out, w_enc, residual, norm_gain):

time: 33 us -> 31.7 us (0.961)
  local copies, waits for them, and re-layouts: 1.33 us -> 0 us
    unnamed x2 -> x0, local copies, waits for them, and re-layouts: 1.33 us -> none
    pallas_call x1, Pallas kernels: 30.9 us -> 29.9 us  [fused(): pl.pallas_call(functools.partial(kernel, n_ctx, n_head, back, CHUNKS), ou...]
    pallas_call x0 -> x1, Pallas kernels: none -> 0.73 us  [fused(): pl.pallas_call(write_out, out_shape=tuple((pltpu.HBM(one.shape, one.dtype...]
where the time goes in v2:
time: 31.7 us; the launch traced here: 31.3 us
  Pallas kernels  30.7 us (97%)
  between operations  0.64 us (2%)
    pallas_call x1, Pallas kernels, fused(): pl.pallas_call(functools.partial(kernel, n_ctx, n_head, back, CHUNKS), ou...  29.9 us
    pallas_call x1, Pallas kernels, fused(): pl.pallas_call(write_out, out_shape=tuple((pltpu.HBM(one.shape, one.dtype...  0.73 us

profile of v2, /device:TPU:4, one launch (start us, length us, event | category | flops | bytes accessed | tf_op | source)
XLA Modules:
  0.0 31.3 jit_solution(5155071034798447352)
XLA Ops:
  0.6 29.9 %latent_layer.1 = (bf16[64,1792]{1,0:T(8,128)(2,1)S(1)}, bf16[64,576]{1,0:T(8,128)(2,1)S(1)}) custom-call(bf16[64,768]{1,0:T(8,128)(2,1)} %q_hbm.1, bf16[64,576]{1,0:T(8,128)(2,1)} %lat_hbm.1, s32[1,64]{1,0:T(1,128)} %bitcast.3, bf16[512,1024]{1,0:T(8,128)(2,1)} %wkv_hbm.1, bf16[512,7168]{1,0:T(8,128)(2,1)} %wout_hbm.1, bf16[576,1792]{1,0:T(8,128)(2,1)} %bitcast.2, ...), custom_call_target="tpu_custom_call" | custom-call | tf_op jit(solution)/shard_map/latent_layer/pallas_call | solution.py:328
  30.6 0.7 %write_out.1 = (bf16[64,1792]{1,0:T(8,128)(2,1)}, bf16[64,576]{1,0:T(8,128)(2,1)}) custom-call(bf16[64,1792]{1,0:T(8,128)(2,1)S(1)} %get-tuple-element.4.attn_v, bf16[64,576]{1,0:T(8,128)(2,1)S(1)} %get-tuple-element.5.next_v), custom_call_target="tpu_custom_call" | custom-call | tf_op jit(solution)/shard_map/write_out/pallas_call | solution.py:365

commit v3 on v2

--- a/solution.py
+++ b/solution.py
@@ -25,13 +25,13 @@
 
 
 def kernel(
-    n_ctx, n_head, back, chunks,
+    n_ctx, n_head, n_rep, back, chunks,
     q_hbm, lat_hbm, doc_hbm, wkv_hbm, wout_hbm, wenc_hbm, res_hbm, gain_hbm,
     attn_ref, next_ref,
     q_v, lat_v, doc_v, wkv_v, wout_v, wenc_v, res_v, gain_v,
     lat_all, att_v, sums_s, sums_r, enc_s, enc_r,
     load_sem, wout_sem, lat_send, lat_recv, sums_send, sums_recv,
-    enc_send, enc_recv, far_in,
+    enc_send, enc_recv, far_in, turn,
 ):
     rows = q_hbm.shape[0]
     heads = wkv_hbm.shape[1] // (NOPE + VDIM)
@@ -40,6 +40,7 @@
     pieces = rows // PIECE
     c = lax.axis_index("ctx")
     h = lax.axis_index("head")
+    r = lax.axis_index("rep")
     side = h // 2
     end, mate = 3 * side, 1 + side
     partner = h + 1 - 2 * lax.rem(h, 2)
@@ -59,7 +60,7 @@
         loads[i].start()
 
     barrier = pltpu.get_barrier_semaphore()
-    near = [("ctx", c, step, n_ctx) for step in range(1, back + 1)] + [("head", h, 1, n_head)]
+    near = [("ctx", c, step, n_ctx) for step in range(1, back + 1)] + [("head", h, 1, n_head), ("rep", r, 1, n_rep)]
     for axis, here, step, count in near:
         @pl.when(here + step < count)
         def _():
@@ -69,12 +70,13 @@
         def _():
             pl.semaphore_signal(barrier, inc=1, device_id={axis: here - step}, device_id_type=MESH)
 
+    wout_loads = []
     for role in range(4):
-        for k in range(chunks):
-            start = pl.multiple_of(slices[role] * width + k * part, LANES)
-            pltpu.make_async_copy(
-                wout_hbm.at[:, pl.ds(start, part)], wout_v.at[role, k], wout_sem.at[role]
-            ).start()
+        start = pl.multiple_of(slices[role] * width, LANES)
+        wout_loads.append(pltpu.make_async_copy(
+            wout_hbm.at[:, pl.ds(start, width)], wout_v.at[role], wout_sem.at[role]
+        ))
+        wout_loads[-1].start()
     for i in range(4, 7):
         loads[i].start()
 
@@ -148,35 +150,52 @@
     kv_own = expand(lat_v[:, :KVL])
     own = score(kv_own, lat_all[back, :, KVL:], seen_own)
 
-    for step in range(1, back + 1):
-        @pl.when(c >= step)
-        def _():
-            latent_copy(step).wait_recv()
-
-    count = back * rows
-    tail_prev = lat_all[:back, :, KVL:].reshape(count, LANES)
-    pick = (lax.broadcasted_iota(jnp.int32, (16, LANES), 1) == ROPE).astype(jnp.float32).astype(jnp.bfloat16)
-    key_docs = lax.dot_general(pick, tail_prev, nt, preferred_element_type=jnp.float32)[0:1]
-    exists = lax.broadcasted_iota(jnp.int32, (rows, count), 1) + (c - back) * rows >= 0
-    seen_prev = (jnp.broadcast_to(key_docs, (rows, count)) == jnp.broadcast_to(doc_col, (rows, count))) & exists
-    kv_prev = expand(lat_all[:back, :, :KVL].reshape(count, KVL))
-    prev = score(kv_prev, tail_prev, seen_prev)
-    for head in range(heads):
-        highest = jnp.maximum(
-            jnp.max(own[head], axis=1, keepdims=True), jnp.max(prev[head], axis=1, keepdims=True)
-        )
-        p_own = jnp.where(seen_own, jnp.exp(own[head] - highest), 0.0)
-        p_prev = jnp.where(seen_prev, jnp.exp(prev[head] - highest), 0.0)
-        total = jnp.sum(p_own, axis=1, keepdims=True) + jnp.sum(p_prev, axis=1, keepdims=True)
-        columns = slice(head * both + NOPE, (head + 1) * both)
-        mixed = jnp.dot(p_own.astype(jnp.bfloat16), kv_own[:, columns], preferred_element_type=jnp.float32)
-        mixed = mixed + jnp.dot(p_prev.astype(jnp.bfloat16), kv_prev[:, columns], preferred_element_type=jnp.float32)
-        att_v[:, head * VDIM : (head + 1) * VDIM] = (mixed / total).astype(jnp.bfloat16)
+
+    def attend(head, weighted, total):
+        att_v[:, head * VDIM : (head + 1) * VDIM] = (weighted / total).astype(jnp.bfloat16)
+
+    def values(expanded, head):
+        return expanded[:, head * both + NOPE : (head + 1) * both]
+
+    def weigh(scores, highest, visible, expanded, head):
+        probs = jnp.where(visible, jnp.exp(scores - highest), 0.0)
+        weighted = jnp.dot(probs.astype(jnp.bfloat16), values(expanded, head), preferred_element_type=jnp.float32)
+        return weighted, jnp.sum(probs, axis=1, keepdims=True)
+
+    @pl.when(c == 0)
+    def _():
+        for head in range(heads):
+            highest = jnp.max(own[head], axis=1, keepdims=True)
+            attend(head, *weigh(own[head], highest, seen_own, kv_own, head))
+
+    @pl.when(c >= 1)
+    def _():
+        for step in range(1, back + 1):
+            @pl.when(c >= step)
+            def _():
+                latent_copy(step).wait_recv()
+
+        count = back * rows
+        tail_prev = lat_all[:back, :, KVL:].reshape(count, LANES)
+        pick = (lax.broadcasted_iota(jnp.int32, (16, LANES), 1) == ROPE).astype(jnp.float32).astype(jnp.bfloat16)
+        key_docs = lax.dot_general(pick, tail_prev, nt, preferred_element_type=jnp.float32)[0:1]
+        exists = lax.broadcasted_iota(jnp.int32, (rows, count), 1) + (c - back) * rows >= 0
+        seen_prev = (jnp.broadcast_to(key_docs, (rows, count)) == jnp.broadcast_to(doc_col, (rows, count))) & exists
+        kv_prev = expand(lat_all[:back, :, :KVL].reshape(count, KVL))
+        prev = score(kv_prev, tail_prev, seen_prev)
+        for head in range(heads):
+            highest = jnp.maximum(
+                jnp.max(own[head], axis=1, keepdims=True), jnp.max(prev[head], axis=1, keepdims=True)
+            )
+            here, total_here = weigh(own[head], highest, seen_own, kv_own, head)
+            earlier, total_earlier = weigh(prev[head], highest, seen_prev, kv_prev, head)
+            attend(head, here + earlier, total_here + total_earlier)
+
 
     def partial_of(role, k):
         if k == 0:
-            pltpu.make_async_copy(wout_v.at[role], wout_v.at[role], wout_sem.at[role]).wait()
-        return jnp.dot(att_v[...], wout_v[role, k], preferred_element_type=jnp.float32)
+            wout_loads[role].wait()
+        return jnp.dot(att_v[...], wout_v[role, :, k * part : (k + 1) * part], preferred_element_type=jnp.float32)
 
     def sums_copy(slot, landing, device):
         return pltpu.make_async_remote_copy(
@@ -193,6 +212,9 @@
         )
 
     def finish(k, out, encoded, squares):
+        if k == 0:
+            for i in range(4, 7):
+                loads[i].wait()
         cols = slice(k * part, (k + 1) * part)
         attn_ref[:, cols] = out
         hidden = res_v[:, cols].astype(jnp.float32) + out.astype(jnp.float32)
@@ -216,6 +238,16 @@
     def unpack(packed):
         squares = packed[:, KVL + ROPE : KVL + ROPE + 1] + packed[:, KVL + split : KVL + split + 1]
         return packed[:, : KVL + ROPE], squares
+
+    def give_turn():
+        @pl.when(r + 1 < n_rep)
+        def _():
+            pl.semaphore_signal(turn, inc=1, device_id={"rep": r + 1}, device_id_type=MESH)
+
+    def await_turn():
+        @pl.when(r >= 1)
+        def _():
+            pl.semaphore_wait(turn, 1)
 
     def conclude(near_half):
         for piece in range(pieces):
@@ -227,14 +259,14 @@
             scale = lax.rsqrt(square_sum / (width * n_head) + epsilon)
             next_ref[piece * PIECE : (piece + 1) * PIECE, :] = (whole * scale).astype(jnp.bfloat16)
 
-    for i in range(4, 7):
-        loads[i].wait()
     nothing = jnp.zeros((rows, KVL + ROPE), jnp.float32), jnp.zeros((rows, 1), jnp.float32)
 
     @pl.when(at_end)
     def _():
         for slot in range(3 * chunks):
             role, k = divmod(slot, chunks)
+            if slot == 2 * chunks:
+                await_turn()
             sums_s[slot] = partial_of(role, k).astype(jnp.bfloat16)
             sums_copy(slot, slot, partner).start()
         encoded, squares = nothing
@@ -243,6 +275,8 @@
             sums_copy(k, k, partner).wait_recv()
             mine = mine + sums_r[k].astype(jnp.float32)
             sums_copy(k, chunks + k, partner).wait_recv()
+            if k == 0:
+                give_turn()
             out = (mine + sums_r[chunks + k].astype(jnp.float32)).astype(jnp.bfloat16)
             encoded, squares = finish(k, out, encoded, squares)
         for piece in range(pieces):
@@ -314,7 +348,7 @@
         copy.wait()
 
 
-def fused(n_ctx, n_head, queries, kv_latent, doc_ids, w_kv, w_out, w_enc, residual, norm_gain):
+def fused(n_ctx, n_head, n_rep, queries, kv_latent, doc_ids, w_kv, w_out, w_enc, residual, norm_gain):
     rows = queries.shape[0]
     heads = w_kv.shape[1] // (NOPE + VDIM)
     width = residual.shape[1]
@@ -326,7 +360,7 @@
     vmem = pl.BlockSpec(memory_space=pltpu.VMEM)
     dma = pltpu.SemaphoreType.DMA
     done = pl.pallas_call(
-        functools.partial(kernel, n_ctx, n_head, back, CHUNKS),
+        functools.partial(kernel, n_ctx, n_head, n_rep, back, CHUNKS),
         out_shape=(pltpu.VMEM((rows, width), bf16), pltpu.VMEM((rows, KVL + ROPE), bf16)),
         in_specs=[hbm] * 8,
         out_specs=(vmem, vmem),
@@ -335,7 +369,7 @@
             pltpu.VMEM(kv_latent.shape, bf16),
             pltpu.VMEM((1, rows), jnp.int32),
             pltpu.VMEM(w_kv.shape, bf16),
-            pltpu.VMEM((4, CHUNKS, w_out.shape[0], part), bf16),
+            pltpu.VMEM((4, w_out.shape[0], width), bf16),
             pltpu.VMEM(w_enc.shape[::-1], bf16),
             pltpu.VMEM(residual.shape, bf16),
             pltpu.VMEM((width,), f32),
@@ -354,6 +388,7 @@
             dma,
             dma((2 * pieces,)),
             pltpu.SemaphoreType.REGULAR,
+            pltpu.SemaphoreType.REGULAR,
         ],
         compiler_params=pltpu.CompilerParams(
             collective_id=0, has_side_effects=True, vmem_limit_bytes=VMEM_BYTES
@@ -372,7 +407,7 @@
     )(*[pltpu.with_memory_space_constraint(one, pltpu.VMEM) for one in done])
 
 
-def general(n_ctx, n_head, queries, kv_latent, doc_ids, w_kv, w_out, w_enc, residual, norm_gain):
+def general(n_ctx, n_head, n_rep, queries, kv_latent, doc_ids, w_kv, w_out, w_enc, residual, norm_gain):
     rows_here = queries.shape[0]
     heads_here = w_kv.shape[1] // (NOPE + VDIM)
     query_heads = queries.reshape(rows_here, heads_here, NOPE + ROPE)
@@ -413,16 +448,17 @@
     return (attn_out, next_latent)
 
 
-def per_device(n_ctx, n_head, *args):
+def per_device(n_ctx, n_head, n_rep, *args):
     rows, width = args[6].shape
     whole_tiles = width % (CHUNKS * LANES) == 0 and rows % PIECE == 0 and rows <= LANES
-    body = fused if n_head == 4 and whole_tiles else general
-    return body(n_ctx, n_head, *args)
+    line = n_head == 4 and n_rep == 2
+    body = fused if line and whole_tiles else general
+    return body(n_ctx, n_head, n_rep, *args)
 
 
 def solution(mesh):
     return jax.shard_map(
-        functools.partial(per_device, mesh.shape["ctx"], mesh.shape["head"]),
+        functools.partial(per_device, mesh.shape["ctx"], mesh.shape["head"], mesh.shape["rep"]),
         mesh=mesh,
         in_specs=(
             P(("rep", "ctx"), "head"),

time: 31.7 us -> 30.8 us (0.972)
  Pallas kernels: 30.7 us -> 30 us
    pallas_call x1, Pallas kernels: 29.9 us -> 29.3 us  [fused(): pl.pallas_call(functools.partial(kernel, n_ctx, n_head, n_rep, back, CHUN...]
where the time goes in v3:
time: 30.8 us; the launch traced here: 30.7 us
  Pallas kernels  30 us (97%)
  between operations  0.64 us (2%)
    pallas_call x1, Pallas kernels, fused(): pl.pallas_call(functools.partial(kernel, n_ctx, n_head, n_rep, back, CHUN...  29.3 us
    pallas_call x1, Pallas kernels, fused(): pl.pallas_call(write_out, out_shape=tuple((pltpu.HBM(one.shape, one.dtype...  0.73 us

profile of v3, /device:TPU:4, one launch (start us, length us, event | category | flops | bytes accessed | tf_op | source)
XLA Modules:
  0.0 30.7 jit_solution(9573387045942688598)
XLA Ops:
  0.6 29.3 %latent_layer.1 = (bf16[64,1792]{1,0:T(8,128)(2,1)S(1)}, bf16[64,576]{1,0:T(8,128)(2,1)S(1)}) custom-call(bf16[64,768]{1,0:T(8,128)(2,1)} %q_hbm.1, bf16[64,576]{1,0:T(8,128)(2,1)} %lat_hbm.1, s32[1,64]{1,0:T(1,128)} %bitcast.3, bf16[512,1024]{1,0:T(8,128)(2,1)} %wkv_hbm.1, bf16[512,7168]{1,0:T(8,128)(2,1)} %wout_hbm.1, bf16[576,1792]{1,0:T(8,128)(2,1)} %bitcast.2, ...), custom_call_target="tpu_custom_call" | custom-call | tf_op jit(solution)/shard_map/latent_layer/pallas_call | solution.py:362
  30.0 0.7 %write_out.1 = (bf16[64,1792]{1,0:T(8,128)(2,1)}, bf16[64,576]{1,0:T(8,128)(2,1)}) custom-call(bf16[64,1792]{1,0:T(8,128)(2,1)S(1)} %get-tuple-element.4.attn_v, bf16[64,576]{1,0:T(8,128)(2,1)S(1)} %get-tuple-element.5.next_v), custom_call_target="tpu_custom_call" | custom-call | tf_op jit(solution)/shard_map/write_out/pallas_call | solution.py:400

commit v4 on v3

--- a/solution.py
+++ b/solution.py
@@ -197,10 +197,12 @@
             wout_loads[role].wait()
         return jnp.dot(att_v[...], wout_v[role, :, k * part : (k + 1) * part], preferred_element_type=jnp.float32)
 
+    early = 2 * chunks
+
     def sums_copy(slot, landing, device):
         return pltpu.make_async_remote_copy(
             src_ref=sums_s.at[slot], dst_ref=sums_r.at[landing],
-            send_sem=sums_send, recv_sem=sums_recv.at[landing],
+            send_sem=sums_send.at[0 if slot < early else 1], recv_sem=sums_recv.at[landing],
             device_id={"head": device}, device_id_type=MESH,
         )
 
@@ -239,9 +241,13 @@
         squares = packed[:, KVL + ROPE : KVL + ROPE + 1] + packed[:, KVL + split : KVL + split + 1]
         return packed[:, : KVL + ROPE], squares
 
+    def sent(buffer, sem):
+        pltpu.make_async_copy(buffer, buffer, sem).wait()
+
     def give_turn():
         @pl.when(r + 1 < n_rep)
         def _():
+            sent(sums_s.at[:early], sums_send.at[0])
             pl.semaphore_signal(turn, inc=1, device_id={"rep": r + 1}, device_id_type=MESH)
 
     def await_turn():
@@ -265,18 +271,17 @@
     def _():
         for slot in range(3 * chunks):
             role, k = divmod(slot, chunks)
-            if slot == 2 * chunks:
+            if slot == chunks + 4:
                 await_turn()
             sums_s[slot] = partial_of(role, k).astype(jnp.bfloat16)
             sums_copy(slot, slot, partner).start()
+        give_turn()
         encoded, squares = nothing
         for k in range(chunks):
             mine = partial_of(3, k)
             sums_copy(k, k, partner).wait_recv()
             mine = mine + sums_r[k].astype(jnp.float32)
             sums_copy(k, chunks + k, partner).wait_recv()
-            if k == 0:
-                give_turn()
             out = (mine + sums_r[chunks + k].astype(jnp.float32)).astype(jnp.bfloat16)
             encoded, squares = finish(k, out, encoded, squares)
         for piece in range(pieces):
@@ -323,8 +328,11 @@
         @pl.when(c + step < n_ctx)
         def _():
             latent_copy(step).wait_send()
-    all_sums = pltpu.make_async_copy(sums_s, sums_s, sums_send)
-    all_sums.wait()
+    @pl.when(at_mate | (r + 1 == n_rep))
+    def _():
+        sent(sums_s.at[:early], sums_send.at[0])
+
+    sent(sums_s.at[early:], sums_send.at[1])
     all_pieces = pltpu.make_async_copy(enc_s, enc_s, enc_send)
 
     @pl.when(at_end)
@@ -383,7 +391,7 @@
             dma((4,)),
             dma((back,)),
             dma((back,)),
-            dma,
+            dma((2,)),
             dma((4 * CHUNKS,)),
             dma,
             dma((2 * pieces,)),

time: 30.8 us -> 30.3 us (0.984)
  the two profiles are of different devices: /device:TPU:4 before, /device:TPU:5 now
where the time goes in v4:
time: 30.3 us; the launch traced here: 30.2 us
  Pallas kernels  29.5 us (97%)
  between operations  0.64 us (2%)
    pallas_call x1, Pallas kernels, fused(): pl.pallas_call(functools.partial(kernel, n_ctx, n_head, n_rep, back, CHUN...  28.8 us
    pallas_call x1, Pallas kernels, fused(): pl.pallas_call(write_out, out_shape=tuple((pltpu.HBM(one.shape, one.dtype...  0.73 us

profile of v4, /device:TPU:5, one launch (start us, length us, event | category | flops | bytes accessed | tf_op | source)
XLA Modules:
  0.0 30.2 jit_solution(4333302865799745338)
XLA Ops:
  0.6 28.8 %latent_layer.1 = (bf16[64,1792]{1,0:T(8,128)(2,1)S(1)}, bf16[64,576]{1,0:T(8,128)(2,1)S(1)}) custom-call(bf16[64,768]{1,0:T(8,128)(2,1)} %q_hbm.1, bf16[64,576]{1,0:T(8,128)(2,1)} %lat_hbm.1, s32[1,64]{1,0:T(1,128)} %bitcast.3, bf16[512,1024]{1,0:T(8,128)(2,1)} %wkv_hbm.1, bf16[512,7168]{1,0:T(8,128)(2,1)} %wout_hbm.1, bf16[576,1792]{1,0:T(8,128)(2,1)} %bitcast.2, ...), custom_call_target="tpu_custom_call" | custom-call | tf_op jit(solution)/shard_map/latent_layer/pallas_call | solution.py:370
  29.4 0.7 %write_out.1 = (bf16[64,1792]{1,0:T(8,128)(2,1)}, bf16[64,576]{1,0:T(8,128)(2,1)}) custom-call(bf16[64,1792]{1,0:T(8,128)(2,1)S(1)} %get-tuple-element.4.attn_v, bf16[64,576]{1,0:T(8,128)(2,1)S(1)} %get-tuple-element.5.next_v), custom_call_target="tpu_custom_call" | custom-call | tf_op jit(solution)/shard_map/write_out/pallas_call | solution.py:408

commit v5 on v4

--- a/solution.py
+++ b/solution.py
@@ -197,7 +197,7 @@
             wout_loads[role].wait()
         return jnp.dot(att_v[...], wout_v[role, :, k * part : (k + 1) * part], preferred_element_type=jnp.float32)
 
-    early = 2 * chunks
+    early = 2 * chunks - 1
 
     def sums_copy(slot, landing, device):
         return pltpu.make_async_remote_copy(
@@ -271,7 +271,7 @@
     def _():
         for slot in range(3 * chunks):
             role, k = divmod(slot, chunks)
-            if slot == chunks + 4:
+            if slot == chunks + 3:
                 await_turn()
             sums_s[slot] = partial_of(role, k).astype(jnp.bfloat16)
             sums_copy(slot, slot, partner).start()

time: 30.3 us -> 30.3 us (level)
  no operation moved by 1% of the time
where the time goes in v5:
time: 30.3 us; the launch traced here: 30.2 us
  Pallas kernels  29.5 us (97%)
  between operations  0.64 us (2%)
    pallas_call x1, Pallas kernels, fused(): pl.pallas_call(functools.partial(kernel, n_ctx, n_head, n_rep, back, CHUN...  28.8 us
    pallas_call x1, Pallas kernels, fused(): pl.pallas_call(write_out, out_shape=tuple((pltpu.HBM(one.shape, one.dtype...  0.73 us

profile of v5, /device:TPU:5, one launch (start us, length us, event | category | flops | bytes accessed | tf_op | source)
XLA Modules:
  0.0 30.2 jit_solution(10465523987711316861)
XLA Ops:
  0.6 28.8 %latent_layer.1 = (bf16[64,1792]{1,0:T(8,128)(2,1)S(1)}, bf16[64,576]{1,0:T(8,128)(2,1)S(1)}) custom-call(bf16[64,768]{1,0:T(8,128)(2,1)} %q_hbm.1, bf16[64,576]{1,0:T(8,128)(2,1)} %lat_hbm.1, s32[1,64]{1,0:T(1,128)} %bitcast.3, bf16[512,1024]{1,0:T(8,128)(2,1)} %wkv_hbm.1, bf16[512,7168]{1,0:T(8,128)(2,1)} %wout_hbm.1, bf16[576,1792]{1,0:T(8,128)(2,1)} %bitcast.2, ...), custom_call_target="tpu_custom_call" | custom-call | tf_op jit(solution)/shard_map/latent_layer/pallas_call | solution.py:370
  29.4 0.7 %write_out.1 = (bf16[64,1792]{1,0:T(8,128)(2,1)}, bf16[64,576]{1,0:T(8,128)(2,1)}) custom-call(bf16[64,1792]{1,0:T(8,128)(2,1)S(1)} %get-tuple-element.4.attn_v, bf16[64,576]{1,0:T(8,128)(2,1)S(1)} %get-tuple-element.5.next_v), custom_call_target="tpu_custom_call" | custom-call | tf_op jit(solution)/shard_map/write_out/pallas_call | solution.py:408
